TPU v7x, 32 devices: a whole 2x2x4 slice. The times are simulated.
32 devices in a mesh: row: 8 (over z, core), col: 4 (over y, x).
Axes of the slice: x: 2, y: 2, z: 4, core: 2. Of those that a mesh axis runs over, the one named last changes fastest.
Arguments:
- basis: float32 [8192, 1024], P('row', 'col'), may hold values from -6 to 6
- merge_coef: float32 [1024, 4096], P('row', 'col'), may hold values from -0.1875 to 0.1875
- panels: float32 [2, 8192, 256], P(None, ('row', 'col')), may hold values from -0.0625 to 0.0625
- factors: float32 [2, 256, 256], replicated, may hold values from -1 to 1
Outputs:
- vectors: float32 [8192, 4096], P(('row', 'col'))
- wsum: float32 [2, 256], replicated
All inputs are finite; a program needn't handle non-finite values.
Results may differ from a plain program's by a relative error of at most 0.0001.
Values sent between devices are 32-bit elements; how exact they have to be, the bound alone decides.
No kernel may reach another device: no remote copies, remote signals or barrier semaphores. Data moves between devices by JAX's collectives and lax.ppermute only.
A program may use at most 128 MiB of HBM per device.

v0:
```python
import jax
import jax.numpy as jnp
from jax import lax
from jax.sharding import PartitionSpec as P

HI = lax.Precision.HIGHEST


def matmul(left, right):
    return jnp.dot(left, right, precision=HI, preferred_element_type=jnp.float32)


def to_tall(block):
    return lax.all_to_all(block, "col", split_axis=0, concat_axis=1, tiled=True)


def per_device(basis, merge_coef, panels, factors):
    coef = lax.all_gather(merge_coef, "row", axis=0, tiled=True)
    block = matmul(lax.all_gather(basis, "col", axis=1, tiled=True), coef)
    upper = jnp.triu(factors)
    local_v = lax.all_gather(panels, "col", axis=1, tiled=True)

    def reduce_terms(terms):
        return lax.psum(terms, "row")

    field = block
    first = local_v[0]
    second = local_v[1]
    proj_one = reduce_terms(matmul(first.T, field))
    field = field - matmul(first, matmul(upper[0], proj_one))
    proj_two = reduce_terms(matmul(second.T, field))
    field = field - matmul(second, matmul(upper[1], proj_two))
    row_one = jnp.sum(proj_one, axis=1)
    row_two = jnp.sum(proj_two, axis=1)
    row_one, row_two = lax.psum((row_one, row_two), "col")
    field = to_tall(field)
    scale = jnp.sqrt(jnp.float32(field.shape[1]))
    return (field, jnp.stack([row_one, row_two]) / scale)


def solution(mesh):
    placed = (P("row", "col"), P("row", "col"), P(None, ("row", "col"), None), P())
    return jax.shard_map(
        per_device,
        mesh=mesh,
        in_specs=placed,
        out_specs=(P(("row", "col"), None), P()),
        check_vma=False,
    )
```

profile of v0, /device:TPU:0, one launch (start us, length us, event | category | flops | bytes accessed | tf_op | source)
XLA Modules:
  0.0 370.3 jit_solution(15266776425502628769)
XLA Ops:
  7.2 0.0 all-gather.4.cloned.1.call-start
  7.2 0.7 all-gather.4.cloned.1.call-update
  7.9 0.0 all-gather.6.cloned.1.call-start
  7.9 0.7 all-gather.6.cloned.1.call-update
  8.6 0.0 all-gather.8.cloned.1.call-start
  8.7 0.7 all-gather.8.cloned.1.call-update
  9.4 0.0 all-reduce.4.cloned.1.call-start
  9.4 55.6 %all-gather.4.cloned.1.call-done = f32[1024,1024]{1,0:T(8,128)} async-done(((f32[1024,256]{1,0:T(8,128)}), f32[1024,1024]{1,0:T(8,128)}) %all-gather.4.cloned.1.call-update) | async-done | bytes 4194320 | tf_op jit(solution)/shard_map/all_gather | solution.py:19
  65.0 48.5 %all-gather.6.cloned.1.call-done = f32[1024,1024]{1,0:T(8,128)} async-done(((f32[128,1024]{1,0:T(8,128)}), f32[1024,1024]{1,0:T(8,128)}) %all-gather.6.cloned.1.call-update) | async-done | bytes 4194320 | tf_op jit(solution)/shard_map/all_gather | solution.py:18
  113.5 17.5 %fusion.2 = f32[1024,1024]{1,0:T(8,128)} fusion(f32[1024,1024]{1,0:T(8,128)} %all-gather.4.cloned.1.call-done, f32[1024,1024]{1,0:T(8,128)} %all-gather.6.cloned.1.call-done), kind=kOutput, calls=%fused_computation.14 | convolution fusion | flops 12884901888 | bytes 12582912 | tf_op jit(solution)/shard_map/dot_general | solution.py:10
  131.0 0.0 copy-start.4
  131.0 18.4 %all-gather.8.cloned.1.call-done = f32[2,1024,256]{2,1,0:T(8,128)} async-done(((f32[2,256,256]{2,1,0:T(8,128)}), f32[2,1024,256]{2,1,0:T(8,128)}) %all-gather.8.cloned.1.call-update) | async-done | bytes 2097168 | tf_op jit(solution)/shard_map/all_gather | solution.py:21
  149.4 0.0 copy-start.1
  149.4 10.3 %convolution_bitcast_fusion.1 = f32[256,1024]{0,1:T(8,128)} fusion(f32[1024,1024]{1,0:T(8,128)} %fusion.2, f32[2,1024,256]{2,1,0:T(8,128)} %all-gather.8.cloned.1.call-done), kind=kOutput, calls=%fused_computation.3 | convolution fusion | flops 3221225472 | bytes 6291456 | tf_op jit(solution)/shard_map/dot_general | solution.py:10
  159.7 0.0 all-reduce.4.cloned.1.call-update
  159.7 0.0 all-reduce.6.cloned.1.call-start
  159.8 0.1 iota_compare_fusion
  159.9 0.0 copy-done.4
  159.9 0.1 broadcast_select_fusion
  159.9 59.2 %all-reduce.4.cloned.1.call-done = f32[256,1024]{0,1:T(8,128)} async-done(((f32[256,1024]{0,1:T(8,128)}), f32[256,1024]{0,1:T(8,128)}) %all-reduce.4.cloned.1.call-update) | async-done | bytes 1048592 | tf_op jit(solution)/shard_map/psum | solution.py:24
  219.2 2.3 fusion.1
  221.4 0.0 copy-done.1
  221.4 5.7 %bitcast_subtract_fusion.1 = f32[1024,1024]{1,0:T(8,128)S(1)} fusion(f32[1024,1024]{1,0:T(8,128)} %fusion.2, f32[256,1024]{1,0:T(8,128)S(1)} %fusion.1, f32[2,1024,256]{2,1,0:T(8,128)S(1)} %copy-done.1), kind=kOutput, calls=%fused_computation.1 | convolution fusion | flops 3222274048 | bytes 10485760 | tf_op jit(solution)/shard_map/dot_general | solution.py:10
  227.1 0.0 copy-start
  227.1 2.0 copy-done
  229.1 7.8 %convolution_bitcast_fusion = f32[256,1024]{0,1:T(8,128)} fusion(f32[1024,1024]{1,0:T(8,128)S(1)} %bitcast_subtract_fusion.1, f32[2,1024,256]{2,1,0:T(8,128)S(1)} %copy-done.1), kind=kOutput, calls=%fused_computation.2 | convolution fusion | flops 3221225472 | bytes 6291456 | tf_op jit(solution)/shard_map/dot_general | solution.py:10
  237.0 0.0 all-reduce.6.cloned.1.call-update
  237.0 58.5 %all-reduce.6.cloned.1.call-done = f32[256,1024]{0,1:T(8,128)} async-done(((f32[256,1024]{0,1:T(8,128)}), f32[256,1024]{0,1:T(8,128)}) %all-reduce.6.cloned.1.call-update) | async-done | bytes 1048592 | tf_op jit(solution)/shard_map/psum | solution.py:24
  295.5 2.3 fusion
  297.7 6.7 %bitcast_subtract_fusion = f32[1024,1024]{1,0:T(8,128)} fusion(f32[1024,1024]{1,0:T(8,128)} %copy-done, f32[256,1024]{1,0:T(8,128)S(1)} %fusion, f32[2,1024,256]{2,1,0:T(8,128)S(1)} %copy-done.1), kind=kOutput, calls=%fused_computation | convolution fusion | flops 3222274048 | bytes 10485760 | tf_op jit(solution)/shard_map/dot_general | solution.py:10
  304.4 0.0 copy-start.2
  304.4 0.0 copy-start.3
  304.4 5.0 %all-to-all-start = ((f32[4,256,1024]{2,1,0:T(8,128)}), f32[4,256,1024]{2,1,0:T(8,128)}, u32[]{:S(2)}, u32[]{:S(2)}) async-start(f32[4,256,1024]{2,1,0:T(8,128)} %bitcast.36), calls=%async_computation | async-start | bytes 8388608 | tf_op jit(solution)/shard_map/all_to_all | solution.py:14
  309.4 0.0 copy-done.2
  309.4 0.2 reduce_sum.18
  309.6 0.0 copy-done.3
  309.6 0.2 reduce_sum.19
  309.7 48.7 %all-reduce = (f32[1,256]{1,0:T(1,128)S(1)}, f32[1,256]{1,0:T(1,128)S(1)}) all-reduce(f32[1,256]{1,0:T(1,128)S(1)} %bitcast.39, f32[1,256]{1,0:T(1,128)S(1)} %bitcast.38), channel_id=1, replica_groups=mesh['row'=8,'col'=4] {'col'}, use_global_device_ids=true, to_apply=%region_5.6 | all-reduce | flops 512 | bytes 4096 | tf_op jit(solution)/shard_map/psum | solution.py:35
  358.4 0.6 maximum_multiply_fusion
  359.0 0.0 all-to-all-done
  359.0 4.8 %copy.7 = f32[4,32,8,1024]{3,2,0,1:T(8,128)} copy(f32[4,32,8,1024]{3,2,1,0:T(8,128)} %bitcast.12) | data formatting | bytes 8388608 | tf_op jit(solution)/shard_map/all_to_all | solution.py:14
  (1 shorter events, 0.0 us)
Async XLA Ops:
  7.2 57.8 %all-gather.4.cloned.1.call-start = ((), (), s32[]{:S(2)}) async-start(), calls=%async_computation.1 | async-start | bytes 5242880 | tf_op jit(solution)/shard_map/all_gather | solution.py:19
  7.9 105.6 %all-gather.6.cloned.1.call-start = ((), (), s32[]{:S(2)}) async-start(), calls=%async_computation.2 | async-start | bytes 4718592 | tf_op jit(solution)/shard_map/all_gather | solution.py:18
  8.6 140.7 %all-gather.8.cloned.1.call-start = ((), (), s32[]{:S(2)}) async-start(), calls=%async_computation.3 | async-start | bytes 2621440 | tf_op jit(solution)/shard_map/all_gather | solution.py:21
  9.4 209.8 %all-reduce.4.cloned.1.call-start = ((), (), s32[]{:S(2)}) async-start(), calls=%async_computation.4 | async-start | bytes 2097152 | tf_op jit(solution)/shard_map/psum | solution.py:24
  131.0 28.9 %copy-start.4 = (f32[2,256,256]{2,1,0:T(8,128)S(1)}, f32[2,256,256]{2,1,0:T(8,128)}, u32[]{:S(2)}) copy-start(f32[2,256,256]{2,1,0:T(8,128)} %param.7) | copy-start | bytes 1572868
  149.4 72.1 %copy-start.1 = (f32[2,1024,256]{2,1,0:T(8,128)S(1)}, f32[2,1024,256]{2,1,0:T(8,128)}, u32[]{:S(2)}) copy-start(f32[2,1024,256]{2,1,0:T(8,128)} %all-gather.8.cloned.1.call-done) | copy-start | bytes 6291460
  159.7 135.8 %all-reduce.6.cloned.1.call-start = ((), (), s32[]{:S(2)}) async-start(), calls=%async_computation.5 | async-start | bytes 2097152 | tf_op jit(solution)/shard_map/psum | solution.py:24
  227.1 2.0 copy-start
  304.4 5.0 %copy-start.2 = (f32[256,1024]{0,1:T(8,128)S(1)}, f32[256,1024]{0,1:T(8,128)}, u32[]{:S(2)}) copy-start(f32[256,1024]{0,1:T(8,128)} %all-reduce.4.cloned.1.call-done) | copy-start | bytes 3145732
  304.4 5.1 %copy-start.3 = (f32[256,1024]{0,1:T(8,128)S(1)}, f32[256,1024]{0,1:T(8,128)}, u32[]{:S(2)}) copy-start(f32[256,1024]{0,1:T(8,128)} %all-reduce.6.cloned.1.call-done) | copy-start | bytes 3145732
  304.4 54.5 %all-to-all-start = ((f32[4,256,1024]{2,1,0:T(8,128)}), f32[4,256,1024]{2,1,0:T(8,128)}, u32[]{:S(2)}, u32[]{:S(2)}) async-start(f32[4,256,1024]{2,1,0:T(8,128)} %bitcast.36), calls=%async_computation | async-start | bytes 8388608 | tf_op jit(solution)/shard_map/all_to_all | solution.py:14
Sparse Core Ops, SparseCore 0:
  9.8 55.1 all-gather.3
  66.6 46.8 all-gather.5
  115.3 33.9 all-gather.7
  159.8 59.2 all-reduce.3
  237.1 58.2 all-reduce.5
where the time goes:
time: 371 us; the launch traced here: 370 us
  waiting for transfers between devices  242 us (65%)
  matrix products  52.5 us (14%)
  blocking collectives  48.7 us (13%)
  between operations  13.9 us (4%)
  local copies, waits for them, and re-layouts  6.81 us (2%)
  starting transfers between devices  5.16 us (1%)
    psum x2, waiting for transfers between devices, reduce_terms(): return lax.psum(terms, 'row')  118 us
    all_gather x1, waiting for transfers between devices, per_device(): block = matmul(lax.all_gather(basis, 'col', axis=1, tiled=True), coef)  55.6 us
    dot_general x7, matrix products, matmul(): jnp.dot(left, right, precision=HI, preferred_element_type=jnp.float32)  52.5 us
    psum x1, blocking collectives, per_device(): row_one, row_two = lax.psum((row_one, row_two), 'col')  48.7 us
    all_gather x1, waiting for transfers between devices, per_device(): coef = lax.all_gather(merge_coef, 'row', axis=0, tiled=True)  48.5 us
    all_gather x1, waiting for transfers between devices, per_device(): local_v = lax.all_gather(panels, 'col', axis=1, tiled=True)  18.4 us
  transfers between devices with their start and end apart: 6, of which 5 were waited for; matrix products, arithmetic and copies ran while one was open for 5% of the time, Pallas kernels for 0%

commit v1 on v0

--- a/solution.py
+++ b/solution.py
@@ -4,6 +4,12 @@
 from jax.sharding import PartitionSpec as P
 
 HI = lax.Precision.HIGHEST
+
+
+def stack_and_merge(array, axis, along):
+    parts = lax.all_gather(array, axis, axis=0, tiled=False)
+    out = jnp.concatenate(parts, axis=along)
+    return out
 
 
 def matmul(left, right):
@@ -16,7 +22,7 @@
 
 def per_device(basis, merge_coef, panels, factors):
     coef = lax.all_gather(merge_coef, "row", axis=0, tiled=True)
-    block = matmul(lax.all_gather(basis, "col", axis=1, tiled=True), coef)
+    block = matmul(stack_and_merge(basis, "col", 1), coef)
     upper = jnp.triu(factors)
     local_v = lax.all_gather(panels, "col", axis=1, tiled=True)
 

time: 371 us -> 371 us (level)
  local copies, waits for them, and re-layouts: 6.81 us -> 12.2 us
  waiting for transfers between devices: 242 us -> 237 us
    reshape x0 -> x1, local copies, waits for them, and re-layouts: none -> 5.34 us  [stack_and_merge(): out = jnp.concatenate(parts, axis=along)]
    all_gather x1, waiting for transfers between devices: 48.5 us -> 43.2 us  [per_device(): coef = lax.all_gather(merge_coef, 'row', axis=0, tiled=True)]
  transfers between devices with their start and end apart: 6 -> 6, of which waited for: 5 -> 5; matrix products, arithmetic and copies ran while one was open for 5% -> 6% of each run, Pallas kernels for 0% -> 0%
where the time goes in v1:
time: 371 us; the launch traced here: 370 us
  waiting for transfers between devices  237 us (64%)
  matrix products  52.6 us (14%)
  blocking collectives  48.7 us (13%)
  between operations  13.9 us (4%)
  local copies, waits for them, and re-layouts  12.2 us (3%)
  starting transfers between devices  5.16 us (1%)
    psum x2, waiting for transfers between devices, reduce_terms(): return lax.psum(terms, 'row')  118 us
    all_gather x1, waiting for transfers between devices, stack_and_merge(): parts = lax.all_gather(array, axis, axis=0, tiled=False)  55.7 us
    dot_general x7, matrix products, matmul(): jnp.dot(left, right, precision=HI, preferred_element_type=jnp.float32)  52.6 us
    psum x1, blocking collectives, per_device(): row_one, row_two = lax.psum((row_one, row_two), 'col')  48.7 us
    all_gather x1, waiting for transfers between devices, per_device(): coef = lax.all_gather(merge_coef, 'row', axis=0, tiled=True)  43.2 us
    all_gather x1, waiting for transfers between devices, per_device(): local_v = lax.all_gather(panels, 'col', axis=1, tiled=True)  18.3 us
  transfers between devices with their start and end apart: 6, of which 5 were waited for; matrix products, arithmetic and copies ran while one was open for 6% of the time, Pallas kernels for 0%

profile of v1, /device:TPU:0, one launch (start us, length us, event | category | flops | bytes accessed | tf_op | source)
XLA Modules:
  0.0 370.4 jit_solution(13304061839575053754)
XLA Ops:
  7.2 0.0 all-gather.9.cloned.1.call-start
  7.2 0.7 all-gather.9.cloned.1.call-update
  7.9 0.0 all-gather.5.cloned.1.call-start
  7.9 0.7 all-gather.5.cloned.1.call-update
  8.6 0.0 all-gather.7.cloned.1.call-start
  8.7 0.7 all-gather.7.cloned.1.call-update
  9.4 0.0 all-reduce.4.cloned.1.call-start
  9.4 55.7 %all-gather.9.cloned.1.call-done = f32[4096,256]{1,0:T(8,128)} async-done(((f32[1024,256]{1,0:T(8,128)}), f32[4096,256]{1,0:T(8,128)}) %all-gather.9.cloned.1.call-update) | async-done | bytes 4194320 | tf_op jit(solution)/shard_map/all_gather | solution.py:10
  65.1 5.3 %copy.8 = f32[1024,4,256]{0,2,1:T(8,128)} copy(f32[1024,4,256]{2,0,1:T(8,128)} %bitcast.41) | data formatting | bytes 8388608 | tf_op jit(solution)/shard_map/reshape | solution.py:11
  70.5 43.2 %all-gather.5.cloned.1.call-done = f32[1024,1024]{1,0:T(8,128)} async-done(((f32[128,1024]{1,0:T(8,128)}), f32[1024,1024]{1,0:T(8,128)}) %all-gather.5.cloned.1.call-update) | async-done | bytes 4194320 | tf_op jit(solution)/shard_map/all_gather | solution.py:24
  113.6 17.6 %fusion.2 = f32[1024,1024]{1,0:T(8,128)} fusion(f32[1024,1024]{0,1:T(8,128)} %bitcast.43, f32[1024,1024]{1,0:T(8,128)} %all-gather.5.cloned.1.call-done), kind=kOutput, calls=%fused_computation.14 | convolution fusion | flops 12884901888 | bytes 12582912 | tf_op jit(solution)/shard_map/dot_general | solution.py:16
  131.2 0.0 copy-start.4
  131.2 18.3 %all-gather.7.cloned.1.call-done = f32[2,1024,256]{2,1,0:T(8,128)} async-done(((f32[2,256,256]{2,1,0:T(8,128)}), f32[2,1024,256]{2,1,0:T(8,128)}) %all-gather.7.cloned.1.call-update) | async-done | bytes 2097168 | tf_op jit(solution)/shard_map/all_gather | solution.py:27
  149.5 0.0 copy-start.1
  149.5 10.3 %convolution_bitcast_fusion.1 = f32[256,1024]{0,1:T(8,128)} fusion(f32[1024,1024]{1,0:T(8,128)} %fusion.2, f32[2,1024,256]{2,1,0:T(8,128)} %all-gather.7.cloned.1.call-done), kind=kOutput, calls=%fused_computation.3 | convolution fusion | flops 3221225472 | bytes 6291456 | tf_op jit(solution)/shard_map/dot_general | solution.py:16
  159.8 0.0 all-reduce.4.cloned.1.call-update
  159.8 0.0 all-reduce.6.cloned.1.call-start
  159.9 0.1 iota_compare_fusion
  160.0 0.0 copy-done.4
  160.0 0.1 broadcast_select_fusion
  160.1 59.2 %all-reduce.4.cloned.1.call-done = f32[256,1024]{0,1:T(8,128)} async-done(((f32[256,1024]{0,1:T(8,128)}), f32[256,1024]{0,1:T(8,128)}) %all-reduce.4.cloned.1.call-update) | async-done | bytes 1048592 | tf_op jit(solution)/shard_map/psum | solution.py:30
  219.3 2.3 fusion.1
  221.5 0.0 copy-done.1
  221.6 5.7 %bitcast_subtract_fusion.1 = f32[1024,1024]{1,0:T(8,128)S(1)} fusion(f32[1024,1024]{1,0:T(8,128)} %fusion.2, f32[256,1024]{1,0:T(8,128)S(1)} %fusion.1, f32[2,1024,256]{2,1,0:T(8,128)S(1)} %copy-done.1), kind=kOutput, calls=%fused_computation.1 | convolution fusion | flops 3222274048 | bytes 10485760 | tf_op jit(solution)/shard_map/dot_general | solution.py:16
  227.3 0.0 copy-start
  227.3 2.0 copy-done
  229.3 7.8 %convolution_bitcast_fusion = f32[256,1024]{0,1:T(8,128)} fusion(f32[1024,1024]{1,0:T(8,128)S(1)} %bitcast_subtract_fusion.1, f32[2,1024,256]{2,1,0:T(8,128)S(1)} %copy-done.1), kind=kOutput, calls=%fused_computation.2 | convolution fusion | flops 3221225472 | bytes 6291456 | tf_op jit(solution)/shard_map/dot_general | solution.py:16
  237.1 0.0 all-reduce.6.cloned.1.call-update
  237.2 58.5 %all-reduce.6.cloned.1.call-done = f32[256,1024]{0,1:T(8,128)} async-done(((f32[256,1024]{0,1:T(8,128)}), f32[256,1024]{0,1:T(8,128)}) %all-reduce.6.cloned.1.call-update) | async-done | bytes 1048592 | tf_op jit(solution)/shard_map/psum | solution.py:30
  295.6 2.3 fusion
  297.9 6.7 %bitcast_subtract_fusion = f32[1024,1024]{1,0:T(8,128)} fusion(f32[1024,1024]{1,0:T(8,128)} %copy-done, f32[256,1024]{1,0:T(8,128)S(1)} %fusion, f32[2,1024,256]{2,1,0:T(8,128)S(1)} %copy-done.1), kind=kOutput, calls=%fused_computation | convolution fusion | flops 3222274048 | bytes 10485760 | tf_op jit(solution)/shard_map/dot_general | solution.py:16
  304.6 0.0 copy-start.2
  304.6 0.0 copy-start.3
  304.6 5.0 %all-to-all-start = ((f32[4,256,1024]{2,1,0:T(8,128)}), f32[4,256,1024]{2,1,0:T(8,128)}, u32[]{:S(2)}, u32[]{:S(2)}) async-start(f32[4,256,1024]{2,1,0:T(8,128)} %bitcast.40), calls=%async_computation | async-start | bytes 8388608 | tf_op jit(solution)/shard_map/all_to_all | solution.py:20
  309.5 0.0 copy-done.2
  309.6 0.2 reduce_sum.18
  309.7 0.0 copy-done.3
  309.7 0.2 reduce_sum.19
  309.9 48.7 %all-reduce = (f32[1,256]{1,0:T(1,128)S(1)}, f32[1,256]{1,0:T(1,128)S(1)}) all-reduce(f32[1,256]{1,0:T(1,128)S(1)} %bitcast.45, f32[1,256]{1,0:T(1,128)S(1)} %bitcast.44), channel_id=1, replica_groups=mesh['row'=8,'col'=4] {'col'}, use_global_device_ids=true, to_apply=%region_5.6 | all-reduce | flops 512 | bytes 4096 | tf_op jit(solution)/shard_map/psum | solution.py:41
  358.5 0.6 maximum_multiply_fusion
  359.1 0.0 all-to-all-done
  359.1 4.8 %copy.10 = f32[4,32,8,1024]{3,2,0,1:T(8,128)} copy(f32[4,32,8,1024]{3,2,1,0:T(8,128)} %bitcast.16) | data formatting | bytes 8388608 | tf_op jit(solution)/shard_map/all_to_all | solution.py:20
  (1 shorter events, 0.0 us)
Async XLA Ops:
  7.2 58.0 %all-gather.9.cloned.1.call-start = ((), (), s32[]{:S(2)}) async-start(), calls=%async_computation.5 | async-start | bytes 5242880 | tf_op jit(solution)/shard_map/all_gather | solution.py:10
  7.9 105.7 %all-gather.5.cloned.1.call-start = ((), (), s32[]{:S(2)}) async-start(), calls=%async_computation.1 | async-start | bytes 4718592 | tf_op jit(solution)/shard_map/all_gather | solution.py:24
  8.6 140.9 %all-gather.7.cloned.1.call-start = ((), (), s32[]{:S(2)}) async-start(), calls=%async_computation.2 | async-start | bytes 2621440 | tf_op jit(solution)/shard_map/all_gather | solution.py:27
  9.4 209.9 %all-reduce.4.cloned.1.call-start = ((), (), s32[]{:S(2)}) async-start(), calls=%async_computation.3 | async-start | bytes 2097152 | tf_op jit(solution)/shard_map/psum | solution.py:30
  131.2 28.8 %copy-start.4 = (f32[2,256,256]{2,1,0:T(8,128)S(1)}, f32[2,256,256]{2,1,0:T(8,128)}, u32[]{:S(2)}) copy-start(f32[2,256,256]{2,1,0:T(8,128)} %param.7) | copy-start | bytes 1572868
  149.5 72.0 %copy-start.1 = (f32[2,1024,256]{2,1,0:T(8,128)S(1)}, f32[2,1024,256]{2,1,0:T(8,128)}, u32[]{:S(2)}) copy-start(f32[2,1024,256]{2,1,0:T(8,128)} %all-gather.7.cloned.1.call-done) | copy-start | bytes 6291460
  159.8 135.8 %all-reduce.6.cloned.1.call-start = ((), (), s32[]{:S(2)}) async-start(), calls=%async_computation.4 | async-start | bytes 2097152 | tf_op jit(solution)/shard_map/psum | solution.py:30
  227.3 2.0 copy-start
  304.6 5.0 %copy-start.2 = (f32[256,1024]{0,1:T(8,128)S(1)}, f32[256,1024]{0,1:T(8,128)}, u32[]{:S(2)}) copy-start(f32[256,1024]{0,1:T(8,128)} %all-reduce.4.cloned.1.call-done) | copy-start | bytes 3145732
  304.6 5.1 %copy-start.3 = (f32[256,1024]{0,1:T(8,128)S(1)}, f32[256,1024]{0,1:T(8,128)}, u32[]{:S(2)}) copy-start(f32[256,1024]{0,1:T(8,128)} %all-reduce.6.cloned.1.call-done) | copy-start | bytes 3145732
  304.6 54.6 %all-to-all-start = ((f32[4,256,1024]{2,1,0:T(8,128)}), f32[4,256,1024]{2,1,0:T(8,128)}, u32[]{:S(2)}, u32[]{:S(2)}) async-start(f32[4,256,1024]{2,1,0:T(8,128)} %bitcast.40), calls=%async_computation | async-start | bytes 8388608 | tf_op jit(solution)/shard_map/all_to_all | solution.py:20
Sparse Core Ops, SparseCore 0:
  9.8 55.2 all-gather.8
  66.7 46.8 all-gather.4
  115.5 33.9 all-gather.6
  159.9 59.2 all-reduce.3
  237.3 58.2 all-reduce.5
